TPU v7x, 32 devices: a whole 2x2x4 slice. The times are simulated.
32 devices in a mesh: gx: 8 (over z, y), gy: 4 (over x, core).
Axes of the slice: x: 2, y: 2, z: 4, core: 2. Of those that a mesh axis runs over, the one named last changes fastest.
Arguments:
- snapshots: bfloat16 [8, 8, 4, 2048, 512], P('gx', 'gy'), may hold values from -120 to 120
- basis: bfloat16 [8, 8, 4, 24, 2048], P('gx', 'gy'), may hold values from -0.0625 to 0.0625
- node_counts: int32 [8, 8], P('gx', 'gy'), may hold values from 1024 to 2048, as said below
- adjacency: int32 [8, 8, 3], P('gx', 'gy'), may hold values from 0 to 63, as said below
Outputs:
- operator: float32 [8, 8, 397, 24], P('gx', 'gy')
- reduced_states: float32 [8, 8, 24, 512], P('gx', 'gy')
Inputs may be any that keep to these rules, and one draw needn't show every extreme that they name: Node slot n of subdomain g is live iff n < node_counts[g]; at least 1024 slots are live, and one subdomain has all 2048 live. Subdomain (row, col) has id row * 8 + col. Each row of adjacency holds 3 distinct ids other than its own subdomain's, each within one subdomain row and one subdomain column of it.
All inputs are finite; a program needn't handle non-finite values.
Results may differ from a plain program's by a relative error of at most 0.0003.
Values sent between devices are 32-bit elements; how exact they have to be, the bound alone decides.
A program may use at most 64 MiB of HBM per device.

v0:
```python
import jax
import jax.numpy as jnp
from jax import lax
from jax.sharding import PartitionSpec as P

beta_linear = 0.5
beta_quad = 0.5


def padded_2(cells, sides, width):
    for axis, dim in sides:
        count = lax.axis_size(axis)
        ends = count - 1
        head = lax.slice_in_dim(cells, 0, width, axis=dim)
        tail = lax.slice_in_dim(cells, cells.shape[dim] - width, cells.shape[dim], axis=dim)
        cells = jnp.concatenate(
            [
                lax.ppermute(tail, axis, [(i, (i + 1) % count) for i in range(ends)]),
                cells,
                lax.ppermute(head, axis, [((i + 1) % count, i) for i in range(ends)]),
            ],
            axis=dim,
        )
    return cells


def build_features(state, near):
    ranks = state.shape[1]
    steps = state.shape[2]
    pieces = [
        jnp.ones((state.shape[0], 1, steps), jnp.float32),
        state,
        near.reshape(state.shape[0], -1, steps),
    ]
    for first in range(ranks):
        pieces.append(state[:, first : first + 1] * state[:, first:])
    return jnp.concatenate(pieces, axis=1)


def pick_rows(pieces, links):
    ids = jnp.arange(pieces.shape[0], dtype=jnp.int32)
    hits = (links[:, :, None] == ids[None, None, :]).astype(jnp.float32)
    return jnp.einsum("sbn,nrk->sbrk", hits, pieces, precision=lax.Precision.HIGHEST)


def solve_one(gram, rhs):
    factor = jnp.linalg.cholesky(gram)
    middle = jax.scipy.linalg.solve_triangular(factor, rhs, lower=True)
    return jax.scipy.linalg.solve_triangular(factor, middle, lower=True, trans=1)


def body(snapshots, basis, node_counts, adjacency):
    values = snapshots[0]
    modes = basis[0]
    counts = node_counts[0]
    links = adjacency[0]
    columns = values.shape[0]
    slots = values.shape[2]
    steps = values.shape[3]
    ranks = modes.shape[2]
    live = jnp.arange(slots, dtype=jnp.int32)[None, :] < counts[:, None]
    masked = modes * live.astype(jnp.bfloat16)[:, None, None, :]
    proj = jnp.einsum("svrp,svpk->svrk", masked, values, preferred_element_type=jnp.float32)
    slotsq = jnp.einsum("svpk,svpk->svp", values, values, preferred_element_type=jnp.float32)
    squares = jnp.sum(slotsq * live.astype(jnp.float32)[:, None, :], axis=(0, 2))
    nodes = jnp.sum(counts.astype(jnp.float32))
    total_subs = lax.axis_size("gx") * lax.axis_size("gy") * columns
    grid_cols = columns * lax.axis_size("gy")
    near_row = links // grid_cols
    near_col = links % grid_cols
    local = (near_row - lax.axis_index("gx") + 1) * (columns + 2) + (
        near_col - lax.axis_index("gy") * columns + 1
    )
    cross = jnp.einsum("svrk,swrk->vw", proj, proj, precision=lax.Precision.HIGHEST)
    sq_all, nodes_all, cross_all = lax.psum((squares, nodes, cross), ("gx", "gy"))
    scale = jnp.sqrt(sq_all / (nodes_all * steps) + 1e-06)
    states = jnp.sum(proj / scale[None, :, None, None], axis=1)
    gnorm = jnp.sum(cross_all / (scale[:, None] * scale[None, :])) / (total_subs * ranks * steps)
    padded = padded_2(states[None], (("gx", 0), ("gy", 1)), 1)
    flat = padded.reshape(-1, ranks, steps)
    near = pick_rows(flat, local)
    nbrs = links.shape[1]
    feats = build_features(states, near)
    past = feats[:, :, :-1]
    nlin = 1 + ranks + nbrs * ranks
    nquad = ranks * (ranks + 1) // 2
    reg_diag = steps * jnp.concatenate(
        [
            jnp.full((nlin,), beta_linear, jnp.float32) * gnorm,
            jnp.full((nquad,), beta_quad, jnp.float32) * gnorm * gnorm,
        ]
    )
    gram = (
        jnp.einsum("sfk,sgk->sfg", past, past, precision=lax.Precision.HIGHEST)
        + jnp.diag(reg_diag)[None]
    )
    rhs = jnp.einsum("sfk,srk->sfr", past, states[:, :, 1:], precision=lax.Precision.HIGHEST)
    operator = jax.vmap(solve_one)(gram, rhs)
    return (operator[None], states[None])


def solution(mesh):
    in_specs = (
        P("gx", "gy", None, None, None),
        P("gx", "gy", None, None, None),
        P("gx", "gy"),
        P("gx", "gy", None),
    )
    out_specs = (P("gx", "gy", None, None), P("gx", "gy", None, None))
    return jax.shard_map(body, mesh=mesh, in_specs=in_specs, out_specs=out_specs, check_vma=False)
```

profile of v0, /device:TPU:1, one launch (start us, length us, event | category | flops | bytes accessed | tf_op | source)
XLA Modules:
  0.0 338.8 jit_solution(2032630812765545449)
XLA Ops:
  1.4 7.5 %fusion = f32[2,4,2048]{2,1,0:T(4,128)S(1)} fusion(bf16[1,2,4,2048,512]{4,3,2,1,0:T(8,128)(2,1)} %param.4), kind=kLoop, calls=%fused_computation.3 | loop fusion | flops 25149440 | bytes 16842752 | tf_op jit(solution)/shard_map/svpk,svpk->svp/dot_general | solution.py:64
  8.9 3.2 copy-done
  12.0 3.4 %fusion.1 = f32[2,4,24,512]{3,2,1,0:T(8,128)S(1)} fusion(bf16[1,2,4,2048,512]{4,3,2,1,0:T(8,128)(2,1)S(1)} %copy-done, bf16[1,2,4,24,2048]{4,3,2,1,0:T(8,128)(2,1)} %param.5, bf16[2,2048]{1,0:T(2,128)(2,1)S(1)} %get-tuple-element.61), kind=kOutput, calls=%fused_computation.4 | convolution fusion | flops 403046400 | bytes 17965056 | tf_op jit(solution)/shard_map/svrp,svpk->svrk/dot_general | solution.py:63
  15.5 1.9 convolution_bitcast_fusion
  18.1 40.9 %all-reduce.4 = (f32[4]{0:T(128)S(1)}, f32[]{:T(128)}, f32[4,4]{1,0:T(4,128)S(1)}) all-reduce(f32[4]{0:T(128)S(1)} %multiply_reduce_fusion, f32[]{:T(128)} %convert_reduce_fusion, f32[4,4]{1,0:T(4,128)S(1)} %convolution_bitcast_fusion), channel_id=1, replica_groups=mesh['gx'=8,'gy'=4] {'gx','gy'}, use_global_device_ids=true, to_apply=%region_1.0 | all-reduce | flops 21 | bytes 168 | tf_op jit(solution)/shard_map/psum | solution.py:75
  61.1 4.0 %collective-permute-start = (f32[1,2,24,512]{3,2,1,0:T(8,128)S(1)}, f32[1,2,24,512]{3,2,1,0:T(8,128)S(1)}, u32[]{:S(2)}, u32[]{:S(2)}) collective-permute-start(f32[1,2,24,512]{3,2,1,0:T(8,128)S(1)} %bitcast.156), channel_id=1, source_target_pairs={{0,4},{4,8},{8,12},{12,16},{16,20},{20,24},{24,28},{1,5},{5,9},{9,... | collective-permute-start | bytes 294920 | tf_op jit(solution)/shard_map/ppermute | solution.py:18
  76.7 5.7 %collective-permute-start.2 = (f32[3,1,24,512]{3,2,1,0:T(8,128)S(1)}, f32[3,1,24,512]{3,2,1,0:T(8,128)S(1)}, u32[]{:S(2)}, u32[]{:S(2)}) collective-permute-start(f32[3,1,24,512]{3,2,1,0:T(8,128)S(1)} %get-tuple-element.26), channel_id=1, source_target_pairs={{0,1},{1,2},{2,3},{4,5},{5,6},{6,7},{8,9},{9,10},{10,11},{12,13},{... | collective-permute-start | bytes 442376 | tf_op jit(solution)/shard_map/ppermute | solution.py:18
  82.4 2.1 collective-permute-start.3
  85.8 3.0 collective-permute-done.3
  89.8 8.0 %concatenate.48 = f32[2,397,512]{2,1,0:T(8,128)S(1)} concatenate(f32[2,1,512]{2,1,0:T(1,128)S(1)} %broadcast_in_dim.45, f32[2,24,512]{2,1,0:T(8,128)S(1)} %divide_reduce_fusion, f32[2,72,512]{2,1,0:T(8,128)S(1)} %bitcast.161, f32[2,24,512]{2,1,0:T(8,128)S(1)} %broadcast_multiply_fusion, f32[2,23,512]{2,1,0:T(8,128)S(1)} %slice_multiply_fusion.6, ...), dimensions={1} | concatenate | bytes 3252224 | tf_op jit(solution)/shard_map/concatenate | solution.py:37
  99.3 2.8 fusion.7
  102.9 2.0 fusion.4
  106.1 23.5 %custom-call.38 = f32[2,128,128]{2,1,0:T(8,128)S(1)} custom-call(f32[2,128,128]{2,1,0:T(8,128)S(1)} %cholesky.281), custom_call_target="Cholesky" | custom-call | tf_op jit(solution)/shard_map/vmap(jit(cholesky))/cholesky | solution.py:47
  129.6 19.9 %custom-call.39 = f32[2,1,128,128]{2,3,1,0:T(8,128)S(1)} custom-call(f32[2,1,128,128]{3,2,1,0:T(8,128)S(1)} %select_bitcast_fusion.2), custom_call_target="InvertDiagBlocksLowerTriangular" | custom-call | tf_op jit(solution)/shard_map/vmap(jit(cholesky))/cholesky | solution.py:47
  152.5 23.5 %custom-call.40 = f32[2,128,128]{2,1,0:T(8,128)S(1)} custom-call(f32[2,128,128]{2,1,0:T(8,128)S(1)} %cholesky.285), custom_call_target="Cholesky" | custom-call | tf_op jit(solution)/shard_map/vmap(jit(cholesky))/cholesky | solution.py:47
  175.9 19.7 %custom-call.41 = f32[2,1,128,128]{2,3,1,0:T(8,128)S(1)} custom-call(f32[2,1,128,128]{3,2,1,0:T(8,128)S(1)} %get-tuple-element.30), custom_call_target="InvertDiagBlocksLowerTriangular" | custom-call | tf_op jit(solution)/shard_map/vmap(jit(cholesky))/cholesky | solution.py:47
  197.3 23.7 %custom-call.42 = f32[2,128,128]{2,1,0:T(8,128)S(1)} custom-call(f32[2,128,128]{2,1,0:T(8,128)S(1)} %cholesky.290), custom_call_target="Cholesky" | custom-call | tf_op jit(solution)/shard_map/vmap(jit(cholesky))/cholesky | solution.py:47
  221.4 19.7 %custom-call.43 = f32[2,1,128,128]{2,3,1,0:T(8,128)S(1)} custom-call(f32[2,1,128,128]{3,2,1,0:T(8,128)S(1)} %get-tuple-element.28), custom_call_target="InvertDiagBlocksLowerTriangular" | custom-call | tf_op jit(solution)/shard_map/vmap(jit(cholesky))/cholesky | solution.py:47
  242.2 2.4 custom-call.44
  246.1 7.9 %while.1 = (s32[]{:T(128)}, f32[2,397,397]{2,1,0:T(8,128)S(1)}, s32[3,2]{0,1:T(2,128)S(1)}, f32[3,2,128,128]{3,2,0,1:T(8,128)}, s32[]{:T(128)}) while((s32[]{:T(128)}, f32[2,397,397]{2,1,0:T(8,128)S(1)}, s32[3,2]{0,1:T(2,128)S(1)}, f32[3,2,128,128]{3,2,0,1:T(8,128)}, s32[]{:T(128)}) %tuple.67), condition=%wide.while_cond, body=%wide.while_body.sunk | while | flops 2 | bytes 263277 | solution.py:49
  246.8 2.0 bitcast_dynamic-update-slice_fusion.2
  249.4 2.0 bitcast_dynamic-update-slice_fusion.2
  252.0 2.0 bitcast_dynamic-update-slice_fusion.2
  255.2 78.6 %custom-call.45 = f32[2,4,128,128]{2,3,1,0:T(8,128)S(1)} custom-call(f32[2,4,128,128]{3,2,1,0:T(8,128)S(1)} %pad_maximum_fusion.1), custom_call_target="InvertDiagBlocksLowerTriangular" | custom-call | tf_op jit(solution)/shard_map/vmap(jit(_solve_triangular))/triangular_solve | solution.py:49
  (130 shorter events, 33.2 us)
Async XLA Ops:
  1.4 10.7 %copy-start = (bf16[1,2,4,2048,512]{4,3,2,1,0:T(8,128)(2,1)S(1)}, bf16[1,2,4,2048,512]{4,3,2,1,0:T(8,128)(2,1)}, u32[]{:S(2)}) copy-start(bf16[1,2,4,2048,512]{4,3,2,1,0:T(8,128)(2,1)} %param.4) | copy-start | bytes 50331652
  12.0 5.5 %copy-start.7 = (s32[1,2]{1,0:T(1,128)S(1)}, s32[1,2]{1,0:T(1,128)}, u32[]{:S(2)}) copy-start(s32[1,2]{1,0:T(1,128)} %param.6) | copy-start | bytes 28
  59.8 38.0 %copy-start.1 = (f32[2,24,512]{2,1,0:T(8,128)}, f32[2,24,512]{2,1,0:T(8,128)S(1)}, u32[]{:S(2)}) copy-start(f32[2,24,512]{2,1,0:T(8,128)S(1)} %divide_reduce_fusion) | copy-start | bytes 294916
  59.8 16.9 %collective-permute-start.1 = (f32[1,2,24,512]{3,2,1,0:T(8,128)S(1)}, f32[1,2,24,512]{3,2,1,0:T(8,128)S(1)}, u32[]{:S(2)}, u32[]{:S(2)}) collective-permute-start(f32[1,2,24,512]{3,2,1,0:T(8,128)S(1)} %bitcast.155), channel_id=1, source_target_pairs={{4,0},{8,4},{12,8},{16,12},{20,16},{24,20},{28,24},{5,1},{9,5},{13... | collective-permute-start | bytes 294920 | tf_op jit(solution)/shard_map/ppermute | solution.py:20
  61.1 15.6 %collective-permute-start = (f32[1,2,24,512]{3,2,1,0:T(8,128)S(1)}, f32[1,2,24,512]{3,2,1,0:T(8,128)S(1)}, u32[]{:S(2)}, u32[]{:S(2)}) collective-permute-start(f32[1,2,24,512]{3,2,1,0:T(8,128)S(1)} %bitcast.156), channel_id=1, source_target_pairs={{0,4},{4,8},{8,12},{12,16},{16,20},{20,24},{24,28},{1,5},{5,9},{9,... | collective-permute-start | bytes 294920 | tf_op jit(solution)/shard_map/ppermute | solution.py:18
  74.4 1.7 copy-start.6
  76.7 9.1 %collective-permute-start.2 = (f32[3,1,24,512]{3,2,1,0:T(8,128)S(1)}, f32[3,1,24,512]{3,2,1,0:T(8,128)S(1)}, u32[]{:S(2)}, u32[]{:S(2)}) collective-permute-start(f32[3,1,24,512]{3,2,1,0:T(8,128)S(1)} %get-tuple-element.26), channel_id=1, source_target_pairs={{0,1},{1,2},{2,3},{4,5},{5,6},{6,7},{8,9},{9,10},{10,11},{12,13},{... | collective-permute-start | bytes 442376 | tf_op jit(solution)/shard_map/ppermute | solution.py:18
  82.4 6.5 %collective-permute-start.3 = (f32[3,1,24,512]{3,2,1,0:T(8,128)S(1)}, f32[3,1,24,512]{3,2,1,0:T(8,128)S(1)}, u32[]{:S(2)}, u32[]{:S(2)}) collective-permute-start(f32[3,1,24,512]{3,2,1,0:T(8,128)S(1)} %get-tuple-element.27), channel_id=1, source_target_pairs={{1,0},{2,1},{3,2},{5,4},{6,5},{7,6},{9,8},{10,9},{11,10},{13,12},{... | collective-permute-start | bytes 442376 | tf_op jit(solution)/shard_map/ppermute | solution.py:20
  104.9 1.2 copy-start.2
  151.0 69.9 %copy-start.4 = (pred[128,128]{1,0:T(8,128)(4,1)S(1)}, pred[128,128]{1,0:T(8,128)(4,1)}, u32[]{:S(2)}) copy-start(pred[128,128]{1,0:T(8,128)(4,1)} %get-tuple-element.87) | copy-start | bytes 49156
  152.4 92.2 %copy-start.5 = (pred[13,13]{1,0:T(8,128)(4,1)S(1)}, pred[13,13]{1,0:T(8,128)(4,1)}, u32[]{:S(2)}) copy-start(pred[13,13]{1,0:T(8,128)(4,1)} %iota_compare_fusion.8) | copy-start | bytes 511
  244.8 1.3 copy-start.8
  244.8 9.2 %copy-start.3 = (f32[128,115]{1,0:T(8,128)S(1)}, f32[128,115]{1,0:T(8,128)}, u32[]{:S(2)}) copy-start(f32[128,115]{1,0:T(8,128)} %pad_convert_fusion) | copy-start | bytes 176644
where the time goes:
time: 344 us; the launch traced here: 339 us
  other arithmetic  236 us (69%)
  blocking collectives  40.9 us (12%)
  local copies, waits for them, and re-layouts  21.6 us (6%)
  matrix products  19.7 us (6%)
  starting transfers between devices  13 us (4%)
  between operations  4.41 us (1%)
    another operation x18, other arithmetic, solve_one(): factor = jnp.linalg.cholesky(gram)  134 us
    another operation x8, other arithmetic, solve_one(): jax.scipy.linalg.solve_triangular(factor, middle, lower=True, trans=1)  83 us
    psum x1, blocking collectives, body(): lax.psum((squares, nodes, cross), ('gx', 'gy'))  40.9 us
    ppermute x2, starting transfers between devices, padded_2(): lax.ppermute(tail, axis, [(i, (i + 1) % count) for i in range(ends)])  9.65 us
    concatenate x1, local copies, waits for them, and re-layouts, build_features(): return jnp.concatenate(pieces, axis=1)  8.01 us
    another operation x9, local copies, waits for them, and re-layouts  7.89 us
    dot_general x1, other arithmetic, body(): jnp.einsum('svpk,svpk->svp', values, values, preferred_element_type=jnp.f...  7.47 us
  transfers between devices with their start and end apart: 4, of which 1 were waited for; matrix products, arithmetic and copies ran while one was open for 3% of the time, Pallas kernels for 0%

commit v1 on v0

--- a/solution.py
+++ b/solution.py
@@ -1,10 +1,15 @@
 import jax
 import jax.numpy as jnp
 from jax import lax
+from jax.experimental import pallas as pl
+from jax.experimental.pallas import tpu as pltpu
 from jax.sharding import PartitionSpec as P
 
 beta_linear = 0.5
 beta_quad = 0.5
+LANES = 128
+SUB = 8
+HIGH = lax.Precision.HIGHEST
 
 
 def padded_2(cells, sides, width):
@@ -24,29 +29,158 @@
     return cells
 
 
-def build_features(state, near):
-    ranks = state.shape[1]
-    steps = state.shape[2]
-    pieces = [
-        jnp.ones((state.shape[0], 1, steps), jnp.float32),
-        state,
-        near.reshape(state.shape[0], -1, steps),
-    ]
-    for first in range(ranks):
-        pieces.append(state[:, first : first + 1] * state[:, first:])
-    return jnp.concatenate(pieces, axis=1)
-
-
 def pick_rows(pieces, links):
     ids = jnp.arange(pieces.shape[0], dtype=jnp.int32)
     hits = (links[:, :, None] == ids[None, None, :]).astype(jnp.float32)
     return jnp.einsum("sbn,nrk->sbrk", hits, pieces, precision=lax.Precision.HIGHEST)
 
 
-def solve_one(gram, rhs):
-    factor = jnp.linalg.cholesky(gram)
-    middle = jax.scipy.linalg.solve_triangular(factor, rhs, lower=True)
-    return jax.scipy.linalg.solve_triangular(factor, middle, lower=True, trans=1)
+def spread_row(tile, row):
+    return jnp.broadcast_to(tile[row : row + 1, :], tile.shape)
+
+
+def spread_lane(tile, lane):
+    if isinstance(lane, int):
+        return jnp.broadcast_to(tile[:, lane : lane + 1], tile.shape)
+    return jnp.take_along_axis(tile, jnp.full(tile.shape, lane, jnp.int32), axis=1)
+
+
+def reduce_panel(tiles, base):
+    sub = lax.broadcasted_iota(jnp.int32, (SUB, LANES), 0)
+    lane = lax.broadcasted_iota(jnp.int32, (SUB, LANES), 1)
+    inside = (lane >= base) & (lane < base + SUB)
+    unit = (lane - base == sub).astype(jnp.float32)
+    count = len(tiles)
+    cols = [[spread_lane(t, base + j) for j in range(SUB)] for t in tiles]
+    tiles = [jnp.where(inside, unit, t) for t in tiles]
+    for j in range(SUB):
+        for s in range(count):
+            here = cols[s][j]
+            inv = 1.0 / spread_row(here, j)
+            row = spread_row(tiles[s], j) * inv
+            tiles[s] = jnp.where(sub == j, row, tiles[s] - here * row)
+            for i in range(j + 1, SUB):
+                row = spread_row(cols[s][i], j) * inv
+                cols[s][i] = jnp.where(sub == j, row, cols[s][i] - here * row)
+    return tiles, inside
+
+
+def clear_rows(tile, base, inside, rows):
+    out = jnp.where(inside, 0.0, tile)
+    terms = [spread_lane(tile, base + j) * rows[j] for j in range(SUB)]
+    while len(terms) > 1:
+        terms = [a + b for a, b in zip(terms[::2], terms[1::2])]
+    return out - terms[0]
+
+
+def mm(a, b):
+    return jnp.dot(a, b, precision=HIGH, preferred_element_type=jnp.float32)
+
+
+def mm_t(a, b):
+    return lax.dot_general(
+        a, b, (((1,), (1,)), ((), ())), precision=HIGH, preferred_element_type=jnp.float32
+    )
+
+
+def fit_kernel(nlin, gnorm_ref, state_ref, near_ref, out_ref, f_ref, tail_ref, m_ref, d_ref):
+    subs, ranks, steps = state_ref.shape
+    nf = out_ref.shape[1]
+    pad = f_ref.shape[1]
+    blocks = nf // LANES
+    head = blocks * LANES
+    rest = pad - head
+    gnorm = gnorm_ref[0]
+    keep = (lax.broadcasted_iota(jnp.int32, (1, steps), 1) < steps - 1).astype(jnp.float32)
+    for s in range(subs):
+        state = state_ref[s]
+        past = state * keep
+        f_ref[s, nf - nf % SUB : pad, :] = jnp.zeros((pad - nf + nf % SUB, steps), jnp.float32)
+        f_ref[s, 0:1, :] = keep
+        f_ref[s, 1 : 1 + ranks, :] = past
+        f_ref[s, 1 + ranks : nlin, :] = near_ref[s] * keep
+        at = nlin
+        for first in range(ranks):
+            f_ref[s, at : at + ranks - first, :] = past[first : first + 1] * state[first:]
+            at += ranks - first
+        tail_ref[s] = jnp.zeros(tail_ref.shape[1:], jnp.float32)
+        tail_ref[s, 0:ranks, :] = pltpu.roll(state, steps - 1, 1)
+        tail_ref[s, ranks : ranks + rest, :] = f_ref[s, head:pad, :]
+    row = lax.broadcasted_iota(jnp.int32, (pad, head + LANES), 0)
+    col = lax.broadcasted_iota(jnp.int32, (pad, head + LANES), 1)
+    level = jnp.where(row < nlin, beta_linear * gnorm, beta_quad * gnorm * gnorm) * steps
+    level = jnp.where(row < nf, level, 1.0)
+    shift = jnp.where(row < head, 0, ranks)
+    ridge = jnp.where(col == row + shift, level, 0.0)
+    for s in range(subs):
+        feats = f_ref[s]
+        m_ref[s, :, 0:head] = mm_t(feats, f_ref[s, 0:head, :]) + ridge[:, 0:head]
+        m_ref[s, :, head:] = mm_t(feats, tail_ref[s]) + ridge[:, head:]
+
+    def block(k, carry):
+        at = pl.multiple_of(k * LANES, LANES)
+        for s in range(subs):
+            d_ref[s] = m_ref[s, pl.ds(at, LANES), pl.ds(at, LANES)]
+
+        def panel(p, carry):
+            base = p * SUB
+            here = pl.ds(pl.multiple_of(base, SUB), SUB)
+            done, inside = reduce_panel([d_ref[s, here, :] for s in range(subs)], base)
+            for s in range(subs):
+                rows = [spread_row(done[s], j) for j in range(SUB)]
+                for r in range(0, LANES, SUB):
+                    d_ref[s, r : r + SUB, :] = clear_rows(d_ref[s, r : r + SUB, :], base, inside, rows)
+                d_ref[s, here, :] = done[s]
+            return carry
+
+        lax.fori_loop(0, LANES // SUB, panel, 0)
+        for s in range(subs):
+            rows = mm(d_ref[s], m_ref[s, pl.ds(at, LANES), :])
+            m_ref[s] = m_ref[s] - mm(m_ref[s, :, pl.ds(at, LANES)], rows)
+            m_ref[s, pl.ds(at, LANES), :] = rows
+        return carry
+
+    lax.fori_loop(0, blocks, block, 0)
+    groups = rest // SUB
+    tiles = [[m_ref[s, head + SUB * g : head + SUB * g + SUB, head:] for g in range(groups)] for s in range(subs)]
+    for p in range(groups):
+        base = ranks + p * SUB
+        done, inside = reduce_panel([tiles[s][p] for s in range(subs)], base)
+        for s in range(subs):
+            rows = [spread_row(done[s], j) for j in range(SUB)]
+            tiles[s] = [done[s] if g == p else clear_rows(tiles[s][g], base, inside, rows) for g in range(groups)]
+    for s in range(subs):
+        last = jnp.concatenate(tiles[s], axis=0)
+        known = m_ref[s, 0:head, head:]
+        out_ref[s, 0:head, :] = (known - mm(known[:, ranks : ranks + rest], last))[:, 0:ranks]
+        out_ref[s, head:nf, :] = last[0 : nf - head, 0:ranks]
+
+
+def fit(gnorm, states, near):
+    subs, ranks, steps = states.shape
+    nlin = 1 + ranks + near.shape[1]
+    nf = nlin + ranks * (ranks + 1) // 2
+    pad = -(-nf // SUB) * SUB
+    head = nf // LANES * LANES
+
+    def kernel(*refs):
+        fit_kernel(nlin, *refs)
+
+    vmem = pl.BlockSpec(memory_space=pltpu.VMEM)
+    return pl.pallas_call(
+        kernel,
+        out_shape=jax.ShapeDtypeStruct((subs, nf, ranks), jnp.float32),
+        in_specs=[pl.BlockSpec(memory_space=pltpu.SMEM), vmem, vmem],
+        out_specs=vmem,
+        scratch_shapes=[
+            pltpu.VMEM((subs, pad, steps), jnp.float32),
+            pltpu.VMEM((subs, LANES, steps), jnp.float32),
+            pltpu.VMEM((subs, pad, head + LANES), jnp.float32),
+            pltpu.VMEM((subs, LANES, LANES), jnp.float32),
+        ],
+        compiler_params=pltpu.CompilerParams(vmem_limit_bytes=40 * 2**20),
+        name="fit",
+    )(gnorm.reshape(1), states, near)
 
 
 def body(snapshots, basis, node_counts, adjacency):
@@ -79,23 +213,7 @@
     padded = padded_2(states[None], (("gx", 0), ("gy", 1)), 1)
     flat = padded.reshape(-1, ranks, steps)
     near = pick_rows(flat, local)
-    nbrs = links.shape[1]
-    feats = build_features(states, near)
-    past = feats[:, :, :-1]
-    nlin = 1 + ranks + nbrs * ranks
-    nquad = ranks * (ranks + 1) // 2
-    reg_diag = steps * jnp.concatenate(
-        [
-            jnp.full((nlin,), beta_linear, jnp.float32) * gnorm,
-            jnp.full((nquad,), beta_quad, jnp.float32) * gnorm * gnorm,
-        ]
-    )
-    gram = (
-        jnp.einsum("sfk,sgk->sfg", past, past, precision=lax.Precision.HIGHEST)
-        + jnp.diag(reg_diag)[None]
-    )
-    rhs = jnp.einsum("sfk,srk->sfr", past, states[:, :, 1:], precision=lax.Precision.HIGHEST)
-    operator = jax.vmap(solve_one)(gram, rhs)
+    operator = fit(gnorm, states, near.reshape(columns, -1, steps))
     return (operator[None], states[None])
 
 

time: 344 us -> 136 us (0.40)
  other arithmetic: 236 us -> 11.6 us
  Pallas kernels: 0 us -> 55.7 us
  local copies, waits for them, and re-layouts: 21.6 us -> 1.6 us
  matrix products: 19.7 us -> 6.07 us
    another operation x26 -> x0, other arithmetic: 217 us -> none  [the longest x18 134 us: solve_one(): factor = jnp.linalg.cholesky(gram)]
    pallas_call x0 -> x1, Pallas kernels: none -> 55.7 us  [fit(): pl.pallas_call(kernel, out_shape=jax.ShapeDtypeStruct((subs, nf, ranks),...]
    another operation x20 -> x0, matrix products: 9.24 us -> none  [the longest x6 5.46 us: solve_one(): factor = jnp.linalg.cholesky(gram)]
    another operation x17 -> x0, local copies, waits for them, and re-layouts: 8.23 us -> none
    concatenate x1 -> x0, local copies, waits for them, and re-layouts: 8.01 us -> none  [build_features(): return jnp.concatenate(pieces, axis=1)]
    mul x25 -> x0, other arithmetic: 5.16 us -> none  [the longest x24 5.16 us: build_features(): pieces.append(state[:, first:first + 1] * state[:, first:])]
    dot_general x2 -> x0, matrix products: 4.33 us -> none  [the longest x1 2.81 us: body(): jnp.einsum('sfk,sgk->sfg', past, past, precision=lax.Precision.HIGHEST)]
  transfers between devices with their start and end apart: 4 -> 4, of which waited for: 1 -> 3; matrix products, arithmetic and copies ran while one was open for 3% -> 1% of each run, Pallas kernels for 0% -> 0%
where the time goes in v1:
time: 136 us; the launch traced here: 134 us
  Pallas kernels  55.7 us (41%)
  blocking collectives  40.9 us (30%)
  starting transfers between devices  13.6 us (10%)
  other arithmetic  11.6 us (9%)
  matrix products  6.07 us (4%)
  waiting for transfers between devices  2.14 us (2%)
  between operations  2.1 us (2%)
  local copies, waits for them, and re-layouts  1.6 us (1%)
    pallas_call x1, Pallas kernels, fit(): pl.pallas_call(kernel, out_shape=jax.ShapeDtypeStruct((subs, nf, ranks),...  55.7 us
    psum x1, blocking collectives, body(): lax.psum((squares, nodes, cross), ('gx', 'gy'))  40.9 us
    dot_general x1, other arithmetic, body(): jnp.einsum('svpk,svpk->svp', values, values, preferred_element_type=jnp.f...  9.1 us
    ppermute x2, starting transfers between devices, padded_2(): lax.ppermute(tail, axis, [(i, (i + 1) % count) for i in range(ends)])  7.53 us
    ppermute x2, starting transfers between devices, padded_2(): lax.ppermute(head, axis, [((i + 1) % count, i) for i in range(ends)])  6.09 us
    dot_general x1, matrix products, body(): jnp.einsum('svrp,svpk->svrk', masked, values, preferred_element_type=jnp....  3.41 us
  transfers between devices with their start and end apart: 4, of which 3 were waited for; matrix products, arithmetic and copies ran while one was open for 1% of the time, Pallas kernels for 0%

profile of v1, /device:TPU:1, one launch (start us, length us, event | category | flops | bytes accessed | tf_op | source)
XLA Modules:
  0.0 133.7 jit_solution(1870558754394513018)
XLA Ops:
  0.6 0.0 copy-start.1
  0.6 0.9 fusion.8
  1.5 0.0 copy-start.3
  1.5 0.0 copy-start.2
  1.6 9.1 %fusion = f32[2,4,2048]{2,1,0:T(4,128)S(1)} fusion(bf16[1,2,4,2048,512]{4,3,2,1,0:T(8,128)(2,1)} %param.4), kind=kLoop, calls=%fused_computation.1 | loop fusion | flops 25149440 | bytes 16842752 | tf_op jit(solution)/shard_map/svpk,svpk->svp/dot_general | solution.py:198
  10.7 0.6 copy-done.1
  11.3 3.4 %fusion.1 = f32[2,4,24,512]{3,2,1,0:T(8,128)S(1)} fusion(bf16[1,2,4,2048,512]{4,3,2,1,0:T(8,128)(2,1)S(1)} %copy-done.1, bf16[1,2,4,24,2048]{4,3,2,1,0:T(8,128)(2,1)} %param.5, bf16[2,2048]{1,0:T(2,128)(2,1)S(1)} %get-tuple-element.12), kind=kOutput, calls=%fused_computation.2 | convolution fusion | flops 403046400 | bytes 17965056 | tf_op jit(solution)/shard_map/svrp,svpk->svrk/dot_general | solution.py:197
  14.7 1.9 %convolution_bitcast_fusion = f32[4,4]{1,0:T(4,128)S(1)} fusion(f32[2,4,24,512]{3,2,1,0:T(8,128)S(1)} %fusion.1), kind=kOutput, calls=%fused_computation.4 | convolution fusion | flops 4718592 | bytes 393280 | tf_op jit(solution)/shard_map/svrk,swrk->vw/dot_general | solution.py:208
  16.6 0.2 multiply_reduce_fusion
  16.8 0.6 convert_reduce_fusion
  17.4 40.9 %all-reduce = (f32[4,4]{1,0:T(4,128)S(1)}, f32[4]{0:T(128)S(1)}, f32[]{:T(128)}) all-reduce(f32[4,4]{1,0:T(4,128)S(1)} %convolution_bitcast_fusion, f32[4]{0:T(128)S(1)} %multiply_reduce_fusion, f32[]{:T(128)} %convert_reduce_fusion), channel_id=1, replica_groups=mesh['gx'=8,'gy'=4] {'gx','gy'}, use_global_device_ids=true, to_apply=%region_0.0 | all-reduce | flops 21 | bytes 168 | tf_op jit(solution)/shard_map/psum | solution.py:209
  58.9 0.1 divide_reduce_fusion.refs_1_
  59.1 1.3 collective-permute-start.1
  60.4 4.0 %collective-permute-start = (f32[1,2,24,512]{3,2,1,0:T(8,128)S(1)}, f32[1,2,24,512]{3,2,1,0:T(8,128)S(1)}, u32[]{:S(2)}, u32[]{:S(2)}) collective-permute-start(f32[1,2,24,512]{3,2,1,0:T(8,128)S(1)} %bitcast.42), channel_id=1, source_target_pairs={{0,4},{4,8},{8,12},{12,16},{16,20},{20,24},{24,28},{1,5},{5,9},{9,... | collective-permute-start | bytes 294920 | tf_op jit(solution)/shard_map/ppermute | solution.py:23
  64.4 0.7 fusion.13
  65.7 0.3 collective-permute-done
  66.0 4.8 %collective-permute-start.3 = (f32[3,1,24,512]{3,2,1,0:T(8,128)S(1)}, f32[3,1,24,512]{3,2,1,0:T(8,128)S(1)}, u32[]{:S(2)}, u32[]{:S(2)}) collective-permute-start(f32[3,1,24,512]{3,2,1,0:T(8,128)S(1)} %get-tuple-element.10), channel_id=1, source_target_pairs={{1,0},{2,1},{3,2},{5,4},{6,5},{7,6},{9,8},{10,9},{11,10},{13,12},{... | collective-permute-start | bytes 442376 | tf_op jit(solution)/shard_map/ppermute | solution.py:25
  70.8 3.5 %collective-permute-start.2 = (f32[3,1,24,512]{3,2,1,0:T(8,128)S(1)}, f32[3,1,24,512]{3,2,1,0:T(8,128)S(1)}, u32[]{:S(2)}, u32[]{:S(2)}) collective-permute-start(f32[3,1,24,512]{3,2,1,0:T(8,128)S(1)} %get-tuple-element.9), channel_id=1, source_target_pairs={{0,1},{1,2},{2,3},{4,5},{5,6},{6,7},{8,9},{9,10},{10,11},{12,13},{... | collective-permute-start | bytes 442376 | tf_op jit(solution)/shard_map/ppermute | solution.py:23
  74.4 0.7 collective-permute-done.3
  75.1 1.2 collective-permute-done.2
  76.3 0.8 fusion.3
  77.1 0.1 copy.14
  77.2 55.7 %fit.1 = f32[2,397,24]{2,1,0:T(8,128)S(1)} custom-call(f32[1]{0:T(128)} %bitcast.5.refs_0_, f32[2,24,512]{2,1,0:T(8,128)S(1)} %divide_reduce_fusion.refs_1_, f32[2,72,512]{2,1,0:T(8,128)S(1)} %bitcast.46), custom_call_target="tpu_custom_call" | custom-call | tf_op jit(solution)/shard_map/fit/pallas_call | solution.py:170
  132.9 0.8 copy.15
  (10 shorter events, 0.1 us)
Async XLA Ops:
  0.6 10.7 %copy-start.1 = (bf16[1,2,4,2048,512]{4,3,2,1,0:T(8,128)(2,1)S(1)}, bf16[1,2,4,2048,512]{4,3,2,1,0:T(8,128)(2,1)}, u32[]{:S(2)}) copy-start(bf16[1,2,4,2048,512]{4,3,2,1,0:T(8,128)(2,1)} %param.4) | copy-start | bytes 50331652
  1.5 15.3 %copy-start.3 = (s32[1,2]{1,0:T(1,128)S(1)}, s32[1,2]{1,0:T(1,128)}, u32[]{:S(2)}) copy-start(s32[1,2]{1,0:T(1,128)} %param.6) | copy-start | bytes 28
  1.5 72.8 %copy-start.2 = (s32[1,2,3]{2,1,0:T(2,128)S(1)}, s32[1,2,3]{2,1,0:T(2,128)}, u32[]{:S(2)}) copy-start(s32[1,2,3]{2,1,0:T(2,128)} %param.7) | copy-start | bytes 76
  59.1 74.6 %copy-start = (f32[2,24,512]{2,1,0:T(8,128)}, f32[2,24,512]{2,1,0:T(8,128)S(1)}, u32[]{:S(2)}) copy-start(f32[2,24,512]{2,1,0:T(8,128)S(1)} %divide_reduce_fusion.refs_1_) | copy-start | bytes 294916
  59.1 6.6 %collective-permute-start.1 = (f32[1,2,24,512]{3,2,1,0:T(8,128)S(1)}, f32[1,2,24,512]{3,2,1,0:T(8,128)S(1)}, u32[]{:S(2)}, u32[]{:S(2)}) collective-permute-start(f32[1,2,24,512]{3,2,1,0:T(8,128)S(1)} %bitcast.41), channel_id=1, source_target_pairs={{4,0},{8,4},{12,8},{16,12},{20,16},{24,20},{28,24},{5,1},{9,5},{13... | collective-permute-start | bytes 294920 | tf_op jit(solution)/shard_map/ppermute | solution.py:25
  60.4 5.6 %collective-permute-start = (f32[1,2,24,512]{3,2,1,0:T(8,128)S(1)}, f32[1,2,24,512]{3,2,1,0:T(8,128)S(1)}, u32[]{:S(2)}, u32[]{:S(2)}) collective-permute-start(f32[1,2,24,512]{3,2,1,0:T(8,128)S(1)} %bitcast.42), channel_id=1, source_target_pairs={{0,4},{4,8},{8,12},{12,16},{16,20},{20,24},{24,28},{1,5},{5,9},{9,... | collective-permute-start | bytes 294920 | tf_op jit(solution)/shard_map/ppermute | solution.py:23
  66.0 9.1 %collective-permute-start.3 = (f32[3,1,24,512]{3,2,1,0:T(8,128)S(1)}, f32[3,1,24,512]{3,2,1,0:T(8,128)S(1)}, u32[]{:S(2)}, u32[]{:S(2)}) collective-permute-start(f32[3,1,24,512]{3,2,1,0:T(8,128)S(1)} %get-tuple-element.10), channel_id=1, source_target_pairs={{1,0},{2,1},{3,2},{5,4},{6,5},{7,6},{9,8},{10,9},{11,10},{13,12},{... | collective-permute-start | bytes 442376 | tf_op jit(solution)/shard_map/ppermute | solution.py:25
  70.8 5.4 %collective-permute-start.2 = (f32[3,1,24,512]{3,2,1,0:T(8,128)S(1)}, f32[3,1,24,512]{3,2,1,0:T(8,128)S(1)}, u32[]{:S(2)}, u32[]{:S(2)}) collective-permute-start(f32[3,1,24,512]{3,2,1,0:T(8,128)S(1)} %get-tuple-element.9), channel_id=1, source_target_pairs={{0,1},{1,2},{2,3},{4,5},{5,6},{6,7},{8,9},{9,10},{10,11},{12,13},{... | collective-permute-start | bytes 442376 | tf_op jit(solution)/shard_map/ppermute | solution.py:23

commit v2 on v1

--- a/solution.py
+++ b/solution.py
@@ -10,29 +10,6 @@
 LANES = 128
 SUB = 8
 HIGH = lax.Precision.HIGHEST
-
-
-def padded_2(cells, sides, width):
-    for axis, dim in sides:
-        count = lax.axis_size(axis)
-        ends = count - 1
-        head = lax.slice_in_dim(cells, 0, width, axis=dim)
-        tail = lax.slice_in_dim(cells, cells.shape[dim] - width, cells.shape[dim], axis=dim)
-        cells = jnp.concatenate(
-            [
-                lax.ppermute(tail, axis, [(i, (i + 1) % count) for i in range(ends)]),
-                cells,
-                lax.ppermute(head, axis, [((i + 1) % count, i) for i in range(ends)]),
-            ],
-            axis=dim,
-        )
-    return cells
-
-
-def pick_rows(pieces, links):
-    ids = jnp.arange(pieces.shape[0], dtype=jnp.int32)
-    hits = (links[:, :, None] == ids[None, None, :]).astype(jnp.float32)
-    return jnp.einsum("sbn,nrk->sbrk", hits, pieces, precision=lax.Precision.HIGHEST)
 
 
 def spread_row(tile, row):
@@ -83,14 +60,15 @@
     )
 
 
-def fit_kernel(nlin, gnorm_ref, state_ref, near_ref, out_ref, f_ref, tail_ref, m_ref, d_ref):
+def fit_kernel(nlin, gnorm_ref, state_ref, near_ref, out_ref, kept_ref, f_ref, tail_ref, m_ref, d_ref):
     subs, ranks, steps = state_ref.shape
     nf = out_ref.shape[1]
     pad = f_ref.shape[1]
     blocks = nf // LANES
     head = blocks * LANES
     rest = pad - head
-    gnorm = gnorm_ref[0]
+    gnorm = gnorm_ref[0:1, 0:1]
+    kept_ref[...] = state_ref[...]
     keep = (lax.broadcasted_iota(jnp.int32, (1, steps), 1) < steps - 1).astype(jnp.float32)
     for s in range(subs):
         state = state_ref[s]
@@ -169,9 +147,12 @@
     vmem = pl.BlockSpec(memory_space=pltpu.VMEM)
     return pl.pallas_call(
         kernel,
-        out_shape=jax.ShapeDtypeStruct((subs, nf, ranks), jnp.float32),
-        in_specs=[pl.BlockSpec(memory_space=pltpu.SMEM), vmem, vmem],
-        out_specs=vmem,
+        out_shape=(
+            jax.ShapeDtypeStruct((subs, nf, ranks), jnp.float32),
+            jax.ShapeDtypeStruct(states.shape, jnp.float32),
+        ),
+        in_specs=[vmem, vmem, vmem],
+        out_specs=(vmem, vmem),
         scratch_shapes=[
             pltpu.VMEM((subs, pad, steps), jnp.float32),
             pltpu.VMEM((subs, LANES, steps), jnp.float32),
@@ -180,40 +161,162 @@
         ],
         compiler_params=pltpu.CompilerParams(vmem_limit_bytes=40 * 2**20),
         name="fit",
-    )(gnorm.reshape(1), states, near)
+    )(gnorm, states, near)
+
+
+def share_kernel(sizes, counts_ref, links_ref, proj_ref, slotsq_ref, near_ref, state_ref, gnorm_ref,
+                 stat_ref, half_ref, row_ref, col_ref, cell_ref, row_sems, col_sems, halo_sems):
+    nx, ny = sizes
+    subs, nvar, ranks, steps = proj_ref.shape
+    slots = slotsq_ref.shape[2]
+    nbrs = links_ref.shape[1]
+    x, y = lax.axis_index("gx"), lax.axis_index("gy")
+    barrier = pltpu.get_barrier_semaphore()
+    sides = [(dx, dy) for dx in (-1, 0, 1) for dy in (-1, 0, 1) if dx or dy]
+
+    def at(dx, dy):
+        return (lax.rem(x + dx + nx, nx), lax.rem(y + dy + ny, ny))
+
+    greeted = [at(d, 0) for d in range(1, nx)] + [at(0, d) for d in range(1, ny)]
+    greeted += [at(dx, dy) for dx, dy in sides if dx and dy]
+    for other in greeted:
+        pl.semaphore_signal(barrier, inc=1, device_id=other, device_id_type=pl.DeviceIdType.MESH)
+
+    pairs = [(v, w) for v in range(nvar) for w in range(v, nvar)]
+    lane = lax.broadcasted_iota(jnp.int32, (1, LANES), 1)
+    stat_ref[...] = jnp.zeros(stat_ref.shape, jnp.float32)
+    squares = jnp.zeros((nvar, LANES), jnp.float32)
+    nodes = 0
+    for s in range(subs):
+        nodes = nodes + counts_ref[s]
+        for p in range(0, slots, LANES):
+            squares += jnp.where(lane + p < counts_ref[s], slotsq_ref[s, :, p : p + LANES], 0.0)
+    stat_ref[0:nvar, :] = squares
+    for i, (v, w) in enumerate(pairs):
+        total = jnp.zeros((ranks, LANES), jnp.float32)
+        for s in range(subs):
+            for k in range(0, steps, LANES):
+                total += proj_ref[s, v, :, k : k + LANES] * proj_ref[s, w, :, k : k + LANES]
+        stat_ref[nvar + i : nvar + i + 1, :] = jnp.sum(total, axis=0, keepdims=True)
+    last = nvar + len(pairs)
+    stat_ref[last : last + 1, :] = jnp.where(lane == 0, nodes.astype(jnp.float32), 0.0)
+
+    pl.semaphore_wait(barrier, len(greeted))
+
+    def gather(src, slots_ref, sems, me, count, step):
+        slots_ref[me] = src[...]
+        copies = []
+        for d in range(1, count):
+            copies.append(
+                pltpu.make_async_remote_copy(
+                    src_ref=src,
+                    dst_ref=slots_ref.at[me],
+                    send_sem=sems.at[0, d],
+                    recv_sem=sems.at[1, d],
+                    device_id=step(d),
+                    device_id_type=pl.DeviceIdType.MESH,
+                )
+            )
+            copies[-1].start()
+        for copy in copies:
+            copy.wait_recv()
+        total = slots_ref[0]
+        for d in range(1, count):
+            total = total + slots_ref[d]
+        return total, copies
+
+    half, sent = gather(stat_ref, row_ref, row_sems, x, nx, lambda d: at(d, 0))
+    half_ref[...] = half
+    total, more = gather(half_ref, col_ref, col_sems, y, ny, lambda d: at(0, d))
+    sent += more
+    total = jnp.broadcast_to(jnp.sum(total, axis=1, keepdims=True), total.shape)
+    nodes = total[last : last + 1, :]
+    scale = [jnp.sqrt(total[v : v + 1, :] / (nodes * steps) + 1e-06) for v in range(nvar)]
+    gnorm = jnp.zeros((1, LANES), jnp.float32)
+    for i, (v, w) in enumerate(pairs):
+        gnorm += (1.0 if v == w else 2.0) * total[nvar + i : nvar + i + 1, :] / (scale[v] * scale[w])
+    gnorm = gnorm / (nx * ny * subs * ranks * steps)
+    gnorm_ref[...] = jnp.broadcast_to(gnorm, gnorm_ref.shape)
+    inverse = [1.0 / part[:, 0:1] for part in scale]
+    wide = subs + 2
+    for s in range(subs):
+        state = proj_ref[s, 0] * inverse[0]
+        for v in range(1, nvar):
+            state = state + proj_ref[s, v] * inverse[v]
+        state_ref[s] = state
+        cell_ref[wide + 1 + s] = state
+    for i, (dx, dy) in enumerate(sides):
+        first, size = (0, subs) if dy == 0 else ((subs - 1, 1) if dy > 0 else (0, 1))
+        into = (1 - dx) * wide + (1 if dy == 0 else (0 if dy > 0 else subs + 1))
+        copy = pltpu.make_async_remote_copy(
+            src_ref=cell_ref.at[pl.ds(wide + 1 + first, size)],
+            dst_ref=cell_ref.at[pl.ds(into, size)],
+            send_sem=halo_sems.at[0, i],
+            recv_sem=halo_sems.at[1, i],
+            device_id=at(dx, dy),
+            device_id_type=pl.DeviceIdType.MESH,
+        )
+        copy.start()
+        sent.append(copy)
+    for i, (dx, dy) in enumerate(sides):
+        sent[len(sent) - len(sides) + i].wait_recv()
+    for copy in sent:
+        copy.wait_send()
+    columns = ny * subs
+    for s in range(subs):
+        for b in range(nbrs):
+            link = links_ref[s, b]
+            row = link // columns
+            cell = (row - x + 1) * wide + link - row * columns - y * subs + 1
+            cell = jnp.clip(cell, 0, 3 * wide - 1)
+            near_ref[s, b * ranks : b * ranks + ranks, :] = cell_ref[cell]
+
+
+def share(counts, links, proj, slotsq):
+    nx, ny = lax.axis_size("gx"), lax.axis_size("gy")
+    subs, nvar, ranks, steps = proj.shape
+    rows = -(-(nvar + nvar * (nvar + 1) // 2 + 1) // SUB) * SUB
+    smem = pl.BlockSpec(memory_space=pltpu.SMEM)
+    vmem = pl.BlockSpec(memory_space=pltpu.VMEM)
+
+    def kernel(*refs):
+        share_kernel((nx, ny), *refs)
+
+    return pl.pallas_call(
+        kernel,
+        out_shape=(
+            jax.ShapeDtypeStruct((subs, links.shape[1] * ranks, steps), jnp.float32),
+            jax.ShapeDtypeStruct((subs, ranks, steps), jnp.float32),
+            jax.ShapeDtypeStruct((SUB, LANES), jnp.float32),
+        ),
+        in_specs=[smem, smem, vmem, vmem],
+        out_specs=(vmem, vmem, vmem),
+        scratch_shapes=[
+            pltpu.VMEM((rows, LANES), jnp.float32),
+            pltpu.VMEM((rows, LANES), jnp.float32),
+            pltpu.VMEM((nx, rows, LANES), jnp.float32),
+            pltpu.VMEM((ny, rows, LANES), jnp.float32),
+            pltpu.VMEM((3 * (subs + 2), ranks, steps), jnp.float32),
+            pltpu.SemaphoreType.DMA((2, nx)),
+            pltpu.SemaphoreType.DMA((2, ny)),
+            pltpu.SemaphoreType.DMA((2, 8)),
+        ],
+        compiler_params=pltpu.CompilerParams(collective_id=0, has_side_effects=True),
+        name="share",
+    )(counts, links, proj, slotsq)
 
 
 def body(snapshots, basis, node_counts, adjacency):
     values = snapshots[0]
     modes = basis[0]
     counts = node_counts[0]
-    links = adjacency[0]
-    columns = values.shape[0]
     slots = values.shape[2]
-    steps = values.shape[3]
-    ranks = modes.shape[2]
     live = jnp.arange(slots, dtype=jnp.int32)[None, :] < counts[:, None]
     masked = modes * live.astype(jnp.bfloat16)[:, None, None, :]
     proj = jnp.einsum("svrp,svpk->svrk", masked, values, preferred_element_type=jnp.float32)
     slotsq = jnp.einsum("svpk,svpk->svp", values, values, preferred_element_type=jnp.float32)
-    squares = jnp.sum(slotsq * live.astype(jnp.float32)[:, None, :], axis=(0, 2))
-    nodes = jnp.sum(counts.astype(jnp.float32))
-    total_subs = lax.axis_size("gx") * lax.axis_size("gy") * columns
-    grid_cols = columns * lax.axis_size("gy")
-    near_row = links // grid_cols
-    near_col = links % grid_cols
-    local = (near_row - lax.axis_index("gx") + 1) * (columns + 2) + (
-        near_col - lax.axis_index("gy") * columns + 1
-    )
-    cross = jnp.einsum("svrk,swrk->vw", proj, proj, precision=lax.Precision.HIGHEST)
-    sq_all, nodes_all, cross_all = lax.psum((squares, nodes, cross), ("gx", "gy"))
-    scale = jnp.sqrt(sq_all / (nodes_all * steps) + 1e-06)
-    states = jnp.sum(proj / scale[None, :, None, None], axis=1)
-    gnorm = jnp.sum(cross_all / (scale[:, None] * scale[None, :])) / (total_subs * ranks * steps)
-    padded = padded_2(states[None], (("gx", 0), ("gy", 1)), 1)
-    flat = padded.reshape(-1, ranks, steps)
-    near = pick_rows(flat, local)
-    operator = fit(gnorm, states, near.reshape(columns, -1, steps))
+    near, states, gnorm = share(counts, adjacency[0], proj, slotsq)
+    operator, states = fit(gnorm, states, near)
     return (operator[None], states[None])
 
 

time: 136 us -> 99.2 us (0.73); the launches traced: 134 us -> 98.9 us
  blocking collectives: 40.9 us -> 0 us
  Pallas kernels: 55.7 us -> 80 us
  starting transfers between devices: 13.6 us -> 0 us
  local copies, waits for them, and re-layouts: 1.6 us -> 4.93 us
  other arithmetic: 11.6 us -> 9.09 us
  waiting for transfers between devices: 2.14 us -> 0 us
  matrix products: 6.07 us -> 4.18 us
  between operations: 2.1 us -> 0.66 us
    psum x1 -> x0, blocking collectives: 40.9 us -> none  [body(): lax.psum((squares, nodes, cross), ('gx', 'gy'))]
    pallas_call x1 -> x2, Pallas kernels: 55.7 us -> 80 us  [the longest x1 55.7 us: fit(): pl.pallas_call(kernel, out_shape=(jax.ShapeDtypeStruct((subs, nf, ranks),...]
    ppermute x4 -> x0, starting transfers between devices: 13.6 us -> none  [the longest x2 7.53 us: padded_2(): lax.ppermute(tail, axis, [(i, (i + 1) % count) for i in range(ends)])]
    unnamed x9, local copies, waits for them, and re-layouts: 1.48 us -> 4.93 us
    dot_general x2 -> x0, matrix products: 2.66 us -> none  [the longest x1 1.9 us: body(): jnp.einsum('svrk,swrk->vw', proj, proj, precision=lax.Precision.HIGHEST)]
    ppermute x4 -> x0, waiting for transfers between devices: 2.14 us -> none  [the longest x2 1.47 us: padded_2(): lax.ppermute(tail, axis, [(i, (i + 1) % count) for i in range(ends)])]
    reduce_sum x4 -> x0, other arithmetic: 1.54 us -> none  [the longest x1 0.68 us: body(): jnp.sum(cross_all / (scale[:, None] * scale[None, :]))]
  transfers between devices with their start and end apart: 4 -> 0, of which waited for: 3 -> 0; matrix products, arithmetic and copies ran while one was open for 1% -> 0% of each run, Pallas kernels for 0% -> 0%
where the time goes in v2:
time: 99.2 us; the launch traced here: 98.9 us
  Pallas kernels  80 us (81%)
  other arithmetic  9.09 us (9%)
  local copies, waits for them, and re-layouts  4.93 us (5%)
  matrix products  4.18 us (4%)
    pallas_call x1, Pallas kernels, fit(): pl.pallas_call(kernel, out_shape=(jax.ShapeDtypeStruct((subs, nf, ranks),...  55.7 us
    pallas_call x1, Pallas kernels, share(): pl.pallas_call(kernel, out_shape=(jax.ShapeDtypeStruct((subs, links.shape...  24.4 us
    dot_general x1, other arithmetic, body(): jnp.einsum('svpk,svpk->svp', values, values, preferred_element_type=jnp.f...  8.21 us
    unnamed x9, local copies, waits for them, and re-layouts  4.93 us
    dot_general x1, matrix products, body(): jnp.einsum('svrp,svpk->svrk', masked, values, preferred_element_type=jnp....  4.18 us

profile of v2, /device:TPU:1, one launch (start us, length us, event | category | flops | bytes accessed | tf_op | source)
XLA Modules:
  0.0 98.9 jit_solution(1108270169830005885)
XLA Ops:
  0.6 0.0 copy-start.3
  0.6 0.9 compare_convert_fusion
  1.5 8.2 %fusion.refs_3_ = f32[2,4,2048]{2,1,0:T(4,128)} fusion(bf16[1,2,4,2048,512]{4,3,2,1,0:T(8,128)(2,1)} %param.4), kind=kLoop, calls=%fused_computation.1 | loop fusion | flops 25149440 | bytes 16842752 | tf_op jit(solution)/shard_map/svpk,svpk->svp/dot_general | solution.py:317
  9.7 1.6 %copy-done.3 = bf16[1,2,4,2048,512]{4,3,2,1,0:T(8,128)(2,1)S(1)} copy-done((bf16[1,2,4,2048,512]{4,3,2,1,0:T(8,128)(2,1)S(1)}, bf16[1,2,4,2048,512]{4,3,2,1,0:T(8,128)(2,1)}, u32[]{:S(2)}) %copy-start.3) | copy-done | bytes 16777240
  11.3 4.2 %fusion.1.refs_2_ = f32[2,4,24,512]{3,2,1,0:T(8,128)} fusion(bf16[1,2,4,2048,512]{4,3,2,1,0:T(8,128)(2,1)S(1)} %copy-done.3, bf16[1,2,4,24,2048]{4,3,2,1,0:T(8,128)(2,1)} %param.5, bf16[2,2048]{1,0:T(2,128)(2,1)S(1)} %compare_convert_fusion), kind=kOutput, calls=%fused_computation.2 | convolution fusion | flops 403046400 | bytes 17965056 | tf_op jit(solution)/shard_map/svrp,svpk->svrk/dot_general | solution.py:316
  15.5 24.4 %share.1 = (f32[2,72,512]{2,1,0:T(8,128)}, f32[2,24,512]{2,1,0:T(8,128)}, f32[8,128]{1,0:T(8,128)}) custom-call(s32[2]{0:T(128)} %bitcast.13, s32[2,3]{1,0:T(2,128)} %bitcast.14, f32[2,4,24,512]{3,2,1,0:T(8,128)} %fusion.1.refs_2_, f32[2,4,2048]{2,1,0:T(4,128)} %fusion.refs_3_), custom_call_target="tpu_custom_call" | custom-call | tf_op jit(solution)/shard_map/share/pallas_call | solution.py:285
  39.9 0.0 copy-start
  39.9 1.0 copy-done
  40.8 0.0 copy-start.1
  40.8 0.9 copy-done.1
  41.7 0.0 copy-start.2
  41.7 0.7 copy-done.2
  42.4 55.7 %fit.1 = (f32[2,397,24]{2,1,0:T(8,128)S(1)}, f32[2,24,512]{2,1,0:T(8,128)}) custom-call(f32[8,128]{1,0:T(8,128)S(1)} %copy-done.2, f32[2,24,512]{2,1,0:T(8,128)S(1)} %copy-done.1, f32[2,72,512]{2,1,0:T(8,128)S(1)} %copy-done), custom_call_target="tpu_custom_call" | custom-call | tf_op jit(solution)/shard_map/fit/pallas_call | solution.py:148
  98.1 0.8 copy.6
Async XLA Ops:
  0.6 10.7 %copy-start.3 = (bf16[1,2,4,2048,512]{4,3,2,1,0:T(8,128)(2,1)S(1)}, bf16[1,2,4,2048,512]{4,3,2,1,0:T(8,128)(2,1)}, u32[]{:S(2)}) copy-start(bf16[1,2,4,2048,512]{4,3,2,1,0:T(8,128)(2,1)} %param.4) | copy-start | bytes 50331652
  39.9 1.0 copy-start
  40.8 0.9 copy-start.1
  41.7 0.7 copy-start.2
